TPU v7x, 32 devices: a whole 2x2x4 slice. The times are simulated.
32 devices in a mesh: rec: 8 (over z, y), vocab: 4 (over x, core).
Axes of the slice: x: 2, y: 2, z: 4, core: 2. Of those that a mesh axis runs over, the one named last changes fastest.
Arguments:
- features: bfloat16 [32, 192, 1280], P('rec'), may hold values from -1000 to 1000
- head_weight: bfloat16 [1280, 32768], P(None, ('vocab', 'rec')), may hold values from -0.15625 to 0.15625
- labels: int32 [32, 128], P('rec'), may hold values from 0 to 32767
- audio_len: int32 [32], P(('rec', 'vocab')), may hold values from 1 to 192, as said below
- transcript_len: int32 [32], P(('rec', 'vocab')), may hold values from 1 to 128
Outputs:
- label_logprob: float32 [32, 192, 128], P(('rec', 'vocab'))
- path_score: float32 [32], P(('rec', 'vocab'))
Inputs may be any that keep to these rules, and one draw needn't show every extreme that they name: `audio_len`: each recording has at least as many frames in use as its transcript has labels.
All inputs are finite; a program needn't handle non-finite values.
Results may differ from a plain program's by a relative error of at most 0.00055.
Values may be sent and summed in bfloat16 or wider, within the bound.
A program may use at most 128 MiB of HBM per device.

v0:
```python
import jax
import jax.numpy as jnp
from jax import lax
from jax.sharding import PartitionSpec as P

negative_fill = -1e30
block_frames = 64


def viterbi(log_prob, audio_len, transcript_len):
    rec_count, frames, slots = log_prob.shape
    states = lax.iota(jnp.int32, slots)[None, :]
    target = states == transcript_len[:, None] - 1
    initial = jnp.where(states == 0, log_prob[:, 0, :], negative_fill)
    best_end = jnp.where(audio_len == 1, jnp.sum(jnp.where(target, initial, 0.0), 1), 0.0)

    def advance(current, emitted):
        shifted = jnp.concatenate(
            [jnp.full_like(current[:, :1], negative_fill), current[:, :-1]], 1
        )
        current = jnp.maximum(current, shifted) + emitted
        return (current, current)

    current = initial
    begin = 1
    while begin < frames:
        finish = min(frames, (begin // block_frames + 1) * block_frames)
        block_in = jnp.moveaxis(log_prob[:, begin:finish, :], 1, 0)
        current, block_scores = lax.scan(advance, current, block_in, unroll=2)
        frame_ids = begin + lax.iota(jnp.int32, finish - begin)
        hit = (frame_ids[:, None] == audio_len[None, :] - 1)[:, :, None] & target[None, :, :]
        reached = jnp.sum(jnp.where(hit, block_scores, 0.0), (0, 2))
        inside = (audio_len - 1 >= begin) & (audio_len - 1 < finish)
        best_end = jnp.where(inside, reached, best_end)
        begin = finish
    return best_end


def body(features, head_weight, labels, audio_len, transcript_len):
    rec_dev, frames, width = features.shape
    frame_rows = features.reshape(rec_dev * frames, width)
    shard_cols = head_weight.shape[1]
    groups = lax.axis_size("rec")
    vocab_count = lax.axis_size("vocab")
    vocab_index = lax.axis_index("vocab")
    gathered = lax.all_gather(head_weight, "rec", axis=1, tiled=True)
    logits = jnp.dot(frame_rows, gathered, preferred_element_type=jnp.float32)
    local_top = jnp.max(logits, 1)
    row_top = lax.pmax(local_top, "vocab")
    row_total = lax.psum(jnp.sum(jnp.exp(logits - row_top[:, None]), 1), "vocab")
    log_norm = (row_top + jnp.log(row_total)).reshape(rec_dev, frames)
    span_cols = shard_cols * groups
    rounded = logits.astype(jnp.bfloat16).reshape(rec_dev, frames, span_cols)
    shard_first = vocab_index * span_cols
    is_owned = (labels >= shard_first) & (labels < shard_first + span_cols)
    position = jnp.where(is_owned, labels - shard_first, -1)
    columns_iota = lax.iota(jnp.int32, span_cols)
    one_hot = (columns_iota[None, :, None] == position[:, None, :]).astype(jnp.bfloat16)
    picked = jnp.einsum("rfv,rvl->rfl", rounded, one_hot, preferred_element_type=jnp.float32)
    own_count = rec_dev // vocab_count
    own_start = vocab_index * own_count
    norm_part = lax.dynamic_slice_in_dim(log_norm, own_start, own_count, 0)
    own_part = lax.psum_scatter(
        picked.astype(jnp.bfloat16), "vocab", scatter_dimension=0, tiled=True
    ).astype(jnp.float32)
    log_prob = own_part - norm_part[:, :, None]
    return (log_prob, viterbi(log_prob, audio_len, transcript_len))


def solution(mesh):
    placed = (
        P("rec", None, None),
        P(None, ("vocab", "rec")),
        P("rec", None),
        P(("rec", "vocab")),
        P(("rec", "vocab")),
    )
    return jax.shard_map(
        body,
        mesh=mesh,
        in_specs=placed,
        out_specs=(P(("rec", "vocab"), None, None), P(("rec", "vocab"))),
        check_vma=False,
    )
```

profile of v0, /device:TPU:11, one launch (start us, length us, event | category | flops | bytes accessed | tf_op | source)
XLA Modules:
  0.0 518.7 jit_solution(1355584377390158057)
XLA Ops:
  7.2 0.7 all-gather.2.cloned.1.call-update
  9.3 0.7 subtract_select_fusion
  10.0 402.6 %all-gather.2.cloned.1.call-done = bf16[1280,8192]{1,0:T(8,128)(2,1)} async-done(((bf16[1280,1024]{1,0:T(8,128)(2,1)}), bf16[1280,8192]{1,0:T(8,128)(2,1)}) %all-gather.2.cloned.1.call-update) | async-done | bytes 20971536 | tf_op jit(solution)/shard_map/all_gather | solution.py:46
  412.6 25.1 %fusion.27 = (f32[768]{0:T(1024)S(1)}, f32[768,8192]{1,0:T(8,128)}) fusion(bf16[768,1280]{1,0:T(8,128)(2,1)S(1)} %bitcast.112, bf16[1280,8192]{1,0:T(8,128)(2,1)} %all-gather.2.cloned.1.call-done), kind=kOutput, calls=%fused_computation.64 | convolution fusion | flops 16112417792 | bytes 48106496 | tf_op jit(solution)/shard_map/dot_general | solution.py:47
  437.7 5.5 %pmax.7 = f32[768]{0:T(1024)S(1)} all-reduce(f32[768]{0:T(1024)S(1)} %get-tuple-element.127), channel_id=1, replica_groups=mesh['rec'=8,'vocab'=4] {'vocab'}, use_global_device_ids=true, to_apply=%region_2.0 | all-reduce | flops 768 | bytes 6144 | tf_op jit(solution)/shard_map/pmax | solution.py:49
  443.1 20.3 %exponential_reduce_fusion = (f32[768]{0:T(1024)S(1)}, bf16[768,8192]{1,0:T(8,128)(2,1)S(1)}) fusion(f32[768,8192]{1,0:T(8,128)} %get-tuple-element.128, f32[768]{0:T(1024)S(1)} %pmax.7), kind=kLoop, calls=%fused_computation.36 | loop fusion | flops 18873600 | bytes 37754880 | tf_op jit(solution)/shard_map/reduce_sum | solution.py:50
  463.4 5.1 fusion.20
  468.7 5.9 %psum.7 = f32[768]{0:T(1024)S(1)} all-reduce(f32[768]{0:T(1024)S(1)} %get-tuple-element.121), channel_id=1, replica_groups=mesh['rec'=8,'vocab'=4] {'vocab'}, use_global_device_ids=true, to_apply=%region_4.5 | all-reduce | flops 768 | bytes 6144 | tf_op jit(solution)/shard_map/psum | solution.py:50
  474.6 0.1 reshape.253
  474.7 12.8 %reduce-scatter.2.cloned.1.call-done = bf16[1,192,128]{2,1,0:T(8,128)(2,1)} async-done(((bf16[4,192,128]{2,1,0:T(8,128)(2,1)}), bf16[1,192,128]{2,1,0:T(8,128)(2,1)}) %reduce-scatter.2.cloned.1.call-update) | async-done | bytes 49168 | tf_op jit(solution)/shard_map/reduce_scatter | solution.py:63
  487.5 0.9 convert_subtract_fusion
  488.5 5.7 %while.36 = (s32[]{:T(128)}, f32[1,128]{1,0:T(1,128)S(1)}, f32[31,2,1,128]{3,1,2,0:T(2,128)S(1)}, f32[31,2,1,128]{3,2,1,0:T(1,128)S(1)}, s32[]{:T(128)}, /*index=5*/f32[1,1]{1,0:T(1,128)}, s32[]{:T(128)}, s32[]{}) while((s32[]{:T(128)}, f32[1,128]{1,0:T(1,128)S(1)}, f32[31,2,1,128]{3,1,2,0:T(2,128)S(1)}, f32[31,2,1,128]{3,2,1,0:T(1,128)S(1)}, ...), condition=%wide.region_6.7_spmd, body=%wide.region_5.6_spmd.sunk | while | flops 1027 | bytes 8313 | solution.py:29
  488.6 0.1 fusion.38
  488.8 0.1 fusion.38
  489.2 0.1 fusion.38
  489.3 0.1 fusion.38
  489.5 0.1 fusion.38
  489.9 0.1 fusion.38
  490.1 0.1 fusion.38
  494.2 0.6 fusion.24
  494.8 5.8 %while.37 = (s32[]{:T(128)}, f32[1,128]{1,0:T(1,128)S(1)}, f32[32,2,1,128]{3,1,2,0:T(2,128)S(1)}, f32[32,2,1,128]{3,2,1,0:T(1,128)S(1)}, s32[]{:T(128)}, /*index=5*/f32[1,1]{1,0:T(1,128)}, s32[]{:T(128)}, s32[]{}) while((s32[]{:T(128)}, f32[1,128]{1,0:T(1,128)S(1)}, f32[32,2,1,128]{3,1,2,0:T(2,128)S(1)}, f32[32,2,1,128]{3,2,1,0:T(1,128)S(1)}, ...), condition=%wide.region_8.9_spmd, body=%wide.region_7.8_spmd.sunk | while | flops 1027 | bytes 8313 | solution.py:29
  500.6 5.8 %while.38 = (s32[]{:T(128)}, f32[1,128]{1,0:T(1,128)S(1)}, f32[32,2,1,128]{3,1,2,0:T(2,128)S(1)}, f32[32,2,1,128]{3,2,1,0:T(1,128)S(1)}, s32[]{:T(128)}, /*index=5*/f32[1,1]{1,0:T(1,128)}, s32[]{:T(128)}, s32[]{}) while((s32[]{:T(128)}, f32[1,128]{1,0:T(1,128)S(1)}, f32[32,2,1,128]{3,1,2,0:T(2,128)S(1)}, f32[32,2,1,128]{3,2,1,0:T(1,128)S(1)}, ...), condition=%wide.region_10.11_spmd, body=%wide.region_9.10_spmd.sunk | while | flops 1027 | bytes 8313 | solution.py:29
  507.1 0.7 fusion.23
  508.5 0.8 fusion.22
  (393 shorter events, 16.3 us)
Async XLA Ops:
  7.2 405.4 %copy-start = (bf16[4,192,1280]{2,1,0:T(8,128)(2,1)S(1)}, bf16[4,192,1280]{2,1,0:T(8,128)(2,1)}, u32[]{:S(2)}) copy-start(bf16[4,192,1280]{2,1,0:T(8,128)(2,1)} %param.11) | copy-start | bytes 5898244
  7.2 405.4 %all-gather.2.cloned.1.call-start = ((), (), s32[]{:S(2)}) async-start(), calls=%async_computation.1 | async-start | bytes 23592960 | tf_op jit(solution)/shard_map/all_gather | solution.py:46
  7.9 479.6 %reduce-scatter.2.cloned.1.call-start = ((), (), s32[]{:S(2)}) async-start(), calls=%async_computation.2 | async-start | bytes 245760 | tf_op jit(solution)/shard_map/reduce_scatter | solution.py:63
  488.4 22.3 %copy-start.1 = (f32[1,192,128]{2,1,0:T(8,128)}, f32[1,192,128]{2,1,0:T(8,128)S(1)}, u32[]{:S(2)}) copy-start(f32[1,192,128]{2,1,0:T(8,128)S(1)} %convert_subtract_fusion) | copy-start | bytes 294916
Sparse Core Ops, SparseCore 0:
  9.5 402.9 all-gather.1
  468.7 18.7 reduce-scatter.1
where the time goes:
time: 522 us; the launch traced here: 519 us
  waiting for transfers between devices  416 us (80%)
  other arithmetic  39.7 us (8%)
  matrix products  30.2 us (6%)
  between operations  19.2 us (4%)
  blocking collectives  11.4 us (2%)
    all_gather x1, waiting for transfers between devices, body(): gathered = lax.all_gather(head_weight, 'rec', axis=1, tiled=True)  403 us
    dot_general x1, matrix products, body(): logits = jnp.dot(frame_rows, gathered, preferred_element_type=jnp.float32)  25.1 us
    reduce_sum x1, other arithmetic, body(): jnp.sum(jnp.exp(logits - row_top[:, None]), 1)  20.3 us
    add x190, other arithmetic, advance(): current = jnp.maximum(current, shifted) + emitted  15 us
    reduce_scatter x1, waiting for transfers between devices, body(): lax.psum_scatter(picked.astype(jnp.bfloat16), 'vocab', scatter_dimension=...  12.8 us
  transfers between devices with their start and end apart: 2, of which 2 were waited for; matrix products, arithmetic and copies ran while one was open for 0% of the time, Pallas kernels for 0%

commit v1 on v0

v1 whole, which is shorter than its diff:
```python
import functools
import jax
import jax.numpy as jnp
from jax import lax
from jax.experimental import pallas as pl
from jax.experimental.pallas import tpu as pltpu
from jax.sharding import PartitionSpec as P

MESH = pl.DeviceIdType.MESH
NEG = -1e30


def flip(v, bit):
    return v + bit * (1 - 2 * ((v // bit) % 2))


def flip_mask(v, mask, bits):
    for bit in bits:
        if mask & bit:
            v = flip(v, bit)
    return v


def gather_kernel(a, b, V, x, w, lab, xo, wo, lo, sw, rw, sl, rl, sf, rf, sg, loc):
    r = lax.axis_index("rec")
    v = lax.axis_index("vocab")
    m, k = r // a, r % a
    own = x.shape[0] // V
    bits = []
    bit = V // 2
    while bit >= 1:
        bits.append(bit)
        bit //= 2
    col_peer = lambda d: (m * a + (k + d) % a, v)
    row_peer = lambda d: (((m + d) % b) * a + k, v)
    barrier = pltpu.get_barrier_semaphore()
    peers = [col_peer(d) for d in range(1, a)] + [row_peer(d) for d in range(1, b)]
    peers += [(r, flip(v, bit)) for bit in bits]
    for peer in peers:
        pl.semaphore_signal(barrier, inc=1, device_id=peer, device_id_type=MESH)
    pl.semaphore_wait(barrier, len(peers))

    def remote(src, dst, ss, rs, to):
        return pltpu.make_async_remote_copy(
            src_ref=src, dst_ref=dst, send_sem=ss, recv_sem=rs, device_id=to, device_id_type=MESH
        )

    sent = []

    def launch(*args):
        c = remote(*args)
        c.start()
        sent.append(c)

    piece = lambda ref, c: ref.at[pl.ds(c * own, own)]
    for d in range(1, b):
        launch(piece(x, v), piece(xo.at[m], v), sf.at[d - 1], rf.at[d - 1, 0], row_peer(d))
    for d in range(1, a):
        launch(w, wo.at[k], sw.at[d - 1], rw.at[d - 1], col_peer(d))
    for d in range(1, b):
        launch(lab, lo.at[m], sl.at[d - 1], rl.at[d - 1], row_peer(d))
    local = [
        pltpu.make_async_copy(x, xo.at[m], loc.at[0]),
        pltpu.make_async_copy(w, wo.at[k], loc.at[1]),
        pltpu.make_async_copy(lab, lo.at[m], loc.at[2]),
    ]
    for c in local:
        c.start()
    order = [0]
    for bit in bits:
        order += [mask | bit for mask in order]
    used = 0
    for mask in order:
        low = (mask & -mask) if mask else V
        c = flip_mask(v, mask, bits)
        for d in range(1, b):
            ms = (m + b - d) % b
            src = piece(xo.at[ms], c)
            remote(src, src, sf.at[d - 1], rf.at[d - 1, mask], row_peer(d)).wait_recv()
            for bit in bits:
                if bit < low:
                    launch(src, src, sg.at[used], rf.at[d - 1, mask | bit], (r, flip(v, bit)))
                    used += 1
    for d in range(1, a):
        ks = (k + a - d) % a
        remote(w, wo.at[ks], sw.at[d - 1], rw.at[d - 1], col_peer(d)).wait_recv()
    for d in range(1, b):
        ms = (m + b - d) % b
        remote(lab, lo.at[ms], sl.at[d - 1], rl.at[d - 1], row_peer(d)).wait_recv()
    for c in sent:
        c.wait_send()
    for c in local:
        c.wait()


def score_kernel(recs, tile, base_ref, x_ref, w_ref, lab_ref, pick_ref, stat_ref, logit):
    a, depth, cols = w_ref.shape
    frames = x_ref.shape[1]
    rows = recs * frames
    xs = x_ref[...].reshape(rows, depth)
    part = None
    acc = [None] * recs
    slots = lab_ref.shape[2]
    for i in range(a):
        for j in range(0, cols, tile):
            l = jnp.dot(xs, w_ref[i, :, j : j + tile], preferred_element_type=jnp.float32)
            at = i * cols + j
            logit[:, at : at + tile] = l
            for n in range(0, tile, 128):
                piece = l[:, n : n + 128]
                part = piece if part is None else jnp.maximum(part, piece)
            low = l.astype(jnp.bfloat16)
            ids = lax.broadcasted_iota(jnp.int32, (tile, slots), 0) + (base_ref[0] + at)
            for q in range(recs):
                hot = (ids == lab_ref[q]).astype(jnp.float32).astype(jnp.bfloat16)
                got = jnp.dot(low[q * frames : (q + 1) * frames], hot, preferred_element_type=jnp.float32)
                acc[q] = got if acc[q] is None else acc[q] + got
    top = jnp.max(part, 1, keepdims=True)
    total = jnp.zeros((rows, 128), jnp.float32)
    for n in range(0, a * cols, 128):
        total = total + jnp.exp(logit[:, n : n + 128] - top)
    total = jnp.sum(total, 1, keepdims=True)
    lane = lax.broadcasted_iota(jnp.int32, (frames, 128), 1)
    for q in range(recs):
        pick_ref[q] = acc[q].astype(jnp.bfloat16)
        part_rows = slice(q * frames, (q + 1) * frames)
        both = jnp.where(lane == 0, top[part_rows], total[part_rows])
        stat_ref[q] = both.T[:8]


def exchange_kernel(a, b, V, pick, stat, po, so, sp, rp, ss, rs, loc):
    r = lax.axis_index("rec")
    v = lax.axis_index("vocab")
    m, k = r // a, r % a
    me = m * V + v
    n = b * V
    peer = lambda d: (((me + d) % n) // V * a + k, (me + d) % V)
    barrier = pltpu.get_barrier_semaphore()
    for d in range(1, n):
        pl.semaphore_signal(barrier, inc=1, device_id=peer(d), device_id_type=MESH)
    pl.semaphore_wait(barrier, n - 1)
    copies = []
    for d in range(1, n):
        to = (me + d) % n
        for src, dst, s, t in ((pick, po, sp, rp), (stat, so, ss, rs)):
            c = pltpu.make_async_remote_copy(
                src_ref=src.at[to], dst_ref=dst.at[me], send_sem=s.at[d - 1], recv_sem=t.at[d - 1],
                device_id=peer(d), device_id_type=MESH,
            )
            c.start()
            copies.append(c)
    local = [
        pltpu.make_async_copy(pick.at[me], po.at[me], loc.at[0]),
        pltpu.make_async_copy(stat.at[me], so.at[me], loc.at[1]),
    ]
    for c in local:
        c.start()
    for d in range(1, n):
        fr = (me + n - d) % n
        for src, dst, s, t in ((pick, po, sp, rp), (stat, so, ss, rs)):
            pltpu.make_async_remote_copy(
                src_ref=src.at[fr], dst_ref=dst.at[fr], send_sem=s.at[d - 1], recv_sem=t.at[d - 1],
                device_id=peer(d), device_id_type=MESH,
            ).wait_recv()
    for c in copies:
        c.wait_send()
    for c in local:
        c.wait()


def align_kernel(alen, tlen, pick, stat, lp_ref, out_ref):
    n, own, frames, slots = pick.shape
    lane = lax.broadcasted_iota(jnp.int32, (1, slots), 1)
    for q in range(own):
        top = stat[0, q, 0:1, :]
        for i in range(1, n):
            top = jnp.maximum(top, stat[i, q, 0:1, :])
        total = jnp.zeros_like(top)
        for i in range(n):
            total = total + stat[i, q, 1:2, :] * jnp.exp(stat[i, q, 0:1, :] - top)
        norm = top + jnp.log(total)
        got = pick[0, q].astype(jnp.float32)
        for i in range(1, n):
            got = got + pick[i, q].astype(jnp.float32)
        lp_ref[q] = got - jnp.broadcast_to(norm, (slots, frames)).T
        last = alen[q] - 1
        first = jnp.where(lane == 0, lp_ref[q, 0:1, :], NEG)

        def advance(t, carry):
            cur, best = carry
            moved = jnp.where(lane == 0, NEG, pltpu.roll(cur, 1, 1))
            cur = jnp.maximum(cur, moved) + lp_ref[q, pl.ds(t, 1), :]
            return cur, jnp.where(last == t, cur, best)

        best = lax.fori_loop(1, frames, advance, (first, first), unroll=4)[1]
        score = jnp.sum(jnp.where(lane == tlen[q] - 1, best, 0.0), 1, keepdims=True)
        out_ref[q] = jnp.broadcast_to(score, (8, 128))


def body(features, head_weight, labels, audio_len, transcript_len):
    rec_dev, frames, width = features.shape
    cols = head_weight.shape[1]
    slots = labels.shape[1]
    G, V = lax.axis_size("rec"), lax.axis_size("vocab")
    best = None
    a = 2
    while a < G:
        cost = (a - 1) * width * cols + (G // a - 1) * features.size
        if G % a == 0 and (best is None or cost < best[0]):
            best = (cost, a)
        a *= 2
    a = best[1]
    b = G // a
    own = rec_dev // V
    vmem = pl.BlockSpec(memory_space=pltpu.VMEM)
    hbm = pl.BlockSpec(memory_space=pl.ANY)
    smem = pl.BlockSpec(memory_space=pltpu.SMEM)
    dma = pltpu.SemaphoreType.DMA
    xg, wg, lg = pl.pallas_call(
        functools.partial(gather_kernel, a, b, V),
        out_shape=(
            jax.ShapeDtypeStruct((b,) + features.shape, features.dtype),
            jax.ShapeDtypeStruct((a,) + head_weight.shape, head_weight.dtype),
            jax.ShapeDtypeStruct((b, rec_dev, 1, slots), jnp.int32),
        ),
        in_specs=[vmem] * 3,
        out_specs=(hbm, hbm, hbm),
        scratch_shapes=[
            dma((a - 1,)), dma((a - 1,)), dma((b - 1,)), dma((b - 1,)),
            dma((b - 1,)), dma((b - 1, V)), dma(((b - 1) * (V - 1),)), dma((3,)),
        ],
        compiler_params=pltpu.CompilerParams(collective_id=0, has_side_effects=True),
        name="gather",
    )(features, head_weight, labels.reshape(rec_dev, 1, slots))

    r, v = lax.axis_index("rec"), lax.axis_index("vocab")
    base = ((v * G + (r // a) * a) * cols).astype(jnp.int32).reshape(1)
    total = b * rec_dev
    recs = 2 if total % 2 == 0 else 1
    tile = min(512, cols)
    pick, stat = pl.pallas_call(
        functools.partial(score_kernel, recs, tile),
        grid=(total // recs,),
        out_shape=(
            jax.ShapeDtypeStruct((total, frames, slots), jnp.bfloat16),
            jax.ShapeDtypeStruct((total, 8, frames), jnp.float32),
        ),
        in_specs=[
            smem,
            pl.BlockSpec((recs, frames, width), lambda i: (i, 0, 0)),
            pl.BlockSpec((a, width, cols), lambda i: (0, 0, 0)),
            pl.BlockSpec((recs, 1, slots), lambda i: (i, 0, 0)),
        ],
        out_specs=(
            pl.BlockSpec((recs, frames, slots), lambda i: (i, 0, 0)),
            pl.BlockSpec((recs, 8, frames), lambda i: (i, 0, 0)),
        ),
        scratch_shapes=[pltpu.VMEM((recs * frames, a * cols), jnp.float32)],
        compiler_params=pltpu.CompilerParams(vmem_limit_bytes=60 * 1024 * 1024),
        name="score",
    )(base, xg.reshape(total, frames, width), wg, lg.reshape(total, 1, slots))

    n = b * V
    pick = pick.reshape(n, own, frames, slots)
    stat = stat.reshape(n, own, 8, frames)
    po, so = pl.pallas_call(
        functools.partial(exchange_kernel, a, b, V),
        out_shape=(
            jax.ShapeDtypeStruct(pick.shape, pick.dtype),
            jax.ShapeDtypeStruct(stat.shape, stat.dtype),
        ),
        in_specs=[vmem] * 2,
        out_specs=(vmem, vmem),
        scratch_shapes=[dma((n - 1,))] * 4 + [dma((2,))],
        compiler_params=pltpu.CompilerParams(collective_id=1, has_side_effects=True),
        name="exchange",
    )(pick, stat)

    log_prob, score = pl.pallas_call(
        align_kernel,
        out_shape=(
            jax.ShapeDtypeStruct((own, frames, slots), jnp.float32),
            jax.ShapeDtypeStruct((own, 8, 128), jnp.float32),
        ),
        in_specs=[smem, smem, vmem, vmem],
        out_specs=(vmem, vmem),
        name="align",
    )(audio_len, transcript_len, po, so)
    return log_prob, score[:, 0, 0]


def solution(mesh):
    return jax.shard_map(
        body,
        mesh=mesh,
        in_specs=(
            P("rec", None, None),
            P(None, ("vocab", "rec")),
            P("rec", None),
            P(("rec", "vocab")),
            P(("rec", "vocab")),
        ),
        out_specs=(P(("rec", "vocab"), None, None), P(("rec", "vocab"))),
        check_vma=False,
    )
```

time: 522 us -> 147 us (0.28)
  waiting for transfers between devices: 416 us -> 0 us
  Pallas kernels: 0 us -> 144 us
  other arithmetic: 39.7 us -> 0 us
  matrix products: 30.2 us -> 0 us
  between operations: 19.2 us -> 1.96 us
  blocking collectives: 11.4 us -> 0 us
    all_gather x1 -> x0, waiting for transfers between devices: 403 us -> none  [body(): gathered = lax.all_gather(head_weight, 'rec', axis=1, tiled=True)]
    pallas_call x0 -> x4, Pallas kernels: none -> 144 us  [the longest x1 62.6 us: body(): pl.pallas_call(functools.partial(gather_kernel, a, b, V), out_shape=(jax....]
    dot_general x2 -> x0, matrix products: 30.2 us -> none  [the longest x1 25.1 us: body(): logits = jnp.dot(frame_rows, gathered, preferred_element_type=jnp.float32)]
    reduce_sum x4 -> x0, other arithmetic: 22.4 us -> none  [the longest x1 20.3 us: body(): jnp.sum(jnp.exp(logits - row_top[:, None]), 1)]
    add x191 -> x0, other arithmetic: 15 us -> none  [the longest x190 15 us: advance(): current = jnp.maximum(current, shifted) + emitted]
    reduce_scatter x1 -> x0, waiting for transfers between devices: 12.8 us -> none  [body(): lax.psum_scatter(picked.astype(jnp.bfloat16), 'vocab', scatter_dimension=...]
    psum x1 -> x0, blocking collectives: 5.94 us -> none  [body(): lax.psum(jnp.sum(jnp.exp(logits - row_top[:, None]), 1), 'vocab')]
    pmax x1 -> x0, blocking collectives: 5.5 us -> none  [body(): row_top = lax.pmax(local_top, 'vocab')]
  transfers between devices with their start and end apart: 2 -> 0, of which waited for: 2 -> 0; matrix products, arithmetic and copies ran while one was open for 0% -> 0% of each run, Pallas kernels for 0% -> 0%
where the time goes in v1:
time: 147 us
  Pallas kernels  144 us (98%)
  between operations  1.96 us (1%)
    pallas_call x1, Pallas kernels, body(): pl.pallas_call(functools.partial(gather_kernel, a, b, V), out_shape=(jax....  62.6 us
    pallas_call x1, Pallas kernels, body(): pl.pallas_call(functools.partial(exchange_kernel, a, b, V), out_shape=(ja...  36.7 us
    pallas_call x1, Pallas kernels, body(): pl.pallas_call(functools.partial(score_kernel, recs, tile), grid=(total /...  29.2 us
    pallas_call x1, Pallas kernels, body(): pl.pallas_call(align_kernel, out_shape=(jax.ShapeDtypeStruct((own, frames...  15.4 us

profile of v1, /device:TPU:11, one launch (start us, length us, event | category | flops | bytes accessed | tf_op | source)
XLA Modules:
  0.0 147.1 jit_solution(11899101975917936127)
XLA Ops:
  0.6 62.6 %gather.1 = (bf16[4,4,192,1280]{3,2,1,0:T(8,128)(2,1)}, bf16[2,1280,1024]{2,1,0:T(8,128)(2,1)}, s32[4,4,1,128]{3,2,1,0:T(1,128)}) custom-call(bf16[4,192,1280]{2,1,0:T(8,128)(2,1)} %x.1, bf16[1280,1024]{1,0:T(8,128)(2,1)} %w.1, s32[4,1,128]{2,1,0:T(1,128)} %bitcast.11), custom_call_target="tpu_custom_call" | custom-call | tf_op jit(solution)/shard_map/gather/pallas_call | solution.py:219
  63.3 29.2 %score.1 = (bf16[16,192,128]{2,1,0:T(8,128)(2,1)}, f32[16,8,192]{2,1,0:T(8,128)}) custom-call(s32[1]{0:T(128)} %bitcast.base_ref, bf16[16,192,1280]{2,1,0:T(8,128)(2,1)} %bitcast.7, bf16[2,1280,1024]{2,1,0:T(8,128)(2,1)} %get-tuple-element.12.w_ref, s32[16,1,128]{2,1,0:T(1,128)} %bitcast.10), custom_call_target="tpu_custom_call" | custom-call | tf_op jit(solution)/shard_map/score/pallas_call | solution.py:241
  92.5 36.7 %exchange.1 = (bf16[16,1,192,128]{3,2,1,0:T(8,128)(2,1)}, f32[16,1,8,192]{3,2,1,0:T(8,128)}) custom-call(bf16[16,1,192,128]{3,2,1,0:T(8,128)(2,1)} %bitcast.8, f32[16,1,8,192]{3,2,1,0:T(8,128)} %bitcast.9), custom_call_target="tpu_custom_call" | custom-call | tf_op jit(solution)/shard_map/exchange/pallas_call | solution.py:266
  130.5 15.4 %align.1 = (f32[1,192,128]{2,1,0:T(8,128)}, f32[1,8,128]{2,1,0:T(8,128)}) custom-call(s32[1]{0:T(128)S(6)} %copy.7.alen, s32[1]{0:T(128)S(6)} %copy.8.tlen, bf16[16,1,192,128]{3,2,1,0:T(8,128)(2,1)} %get-tuple-element.16.pick, f32[16,1,8,192]{3,2,1,0:T(8,128)} %get-tuple-element.17.stat), custom_call_target="tpu_custom_call" | custom-call | tf_op jit(solution)/shard_map/align/pallas_call | solution.py:279
  145.9 1.2 slice.3

commit v2 on v1

--- a/solution.py
+++ b/solution.py
@@ -8,6 +8,7 @@
 
 MESH = pl.DeviceIdType.MESH
 NEG = -1e30
+run = 6
 
 
 def flip(v, bit):
@@ -128,44 +129,55 @@
         stat_ref[q] = both.T[:8]
 
 
-def exchange_kernel(a, b, V, pick, stat, po, so, sp, rp, ss, rs, loc):
+def exchange_kernel(a, b, V, pick, stat, po, so, pin, sin, pout, sout, sp1, rp1, ss1, rs1, sp, rp, ss, rs):
     r = lax.axis_index("rec")
     v = lax.axis_index("vocab")
     m, k = r // a, r % a
-    me = m * V + v
-    n = b * V
-    peer = lambda d: (((me + d) % n) // V * a + k, (me + d) % V)
+    half = V // 2
+    side = v % 2
+    me = m * half + v // 2
+    n = b * half
+    sibling = (r, flip(v, 1))
+    peer = lambda d: (((me + d) % n) // half * a + k, ((me + d) % n) % half * 2 + side)
     barrier = pltpu.get_barrier_semaphore()
-    for d in range(1, n):
-        pl.semaphore_signal(barrier, inc=1, device_id=peer(d), device_id_type=MESH)
-    pl.semaphore_wait(barrier, n - 1)
+    for to in [sibling] + [peer(d) for d in range(1, n)]:
+        pl.semaphore_signal(barrier, inc=1, device_id=to, device_id_type=MESH)
+    pl.semaphore_wait(barrier, n)
+
+    def remote(src, dst, s, t, to):
+        return pltpu.make_async_remote_copy(
+            src_ref=src, dst_ref=dst, send_sem=s, recv_sem=t, device_id=to, device_id_type=MESH
+        )
+
     copies = []
+    for e in range(n):
+        copies.append(remote(pick.at[e, 1 - side], pin.at[e], sp1.at[e], rp1.at[e], sibling))
+        copies.append(remote(stat.at[e, 1 - side], sin.at[e], ss1.at[e], rs1.at[e], sibling))
+    for c in copies:
+        c.start()
+    row = lax.broadcasted_iota(jnp.int32, sin.shape[1:], 1)
+    for e in range(n):
+        copies[2 * e].wait_recv()
+        copies[2 * e + 1].wait_recv()
+        pout[e] = pick[e, side] + pin[e]
+        mine, other = stat[e, side], sin[e]
+        top = jnp.maximum(mine[:, 0:1], other[:, 0:1])
+        total = mine * jnp.exp(mine[:, 0:1] - top) + other * jnp.exp(other[:, 0:1] - top)
+        sout[e] = jnp.where(row == 0, top, total)
     for d in range(1, n):
         to = (me + d) % n
-        for src, dst, s, t in ((pick, po, sp, rp), (stat, so, ss, rs)):
-            c = pltpu.make_async_remote_copy(
-                src_ref=src.at[to], dst_ref=dst.at[me], send_sem=s.at[d - 1], recv_sem=t.at[d - 1],
-                device_id=peer(d), device_id_type=MESH,
-            )
+        for src, dst, s, t in ((pout, po, sp, rp), (sout, so, ss, rs)):
+            c = remote(src.at[to], dst.at[me], s.at[d - 1], t.at[d - 1], peer(d))
             c.start()
             copies.append(c)
-    local = [
-        pltpu.make_async_copy(pick.at[me], po.at[me], loc.at[0]),
-        pltpu.make_async_copy(stat.at[me], so.at[me], loc.at[1]),
-    ]
-    for c in local:
-        c.start()
+    po[me] = pout[me]
+    so[me] = sout[me]
     for d in range(1, n):
         fr = (me + n - d) % n
-        for src, dst, s, t in ((pick, po, sp, rp), (stat, so, ss, rs)):
-            pltpu.make_async_remote_copy(
-                src_ref=src.at[fr], dst_ref=dst.at[fr], send_sem=s.at[d - 1], recv_sem=t.at[d - 1],
-                device_id=peer(d), device_id_type=MESH,
-            ).wait_recv()
+        for src, dst, s, t in ((pout, po, sp, rp), (sout, so, ss, rs)):
+            remote(src.at[fr], dst.at[fr], s.at[d - 1], t.at[d - 1], peer(d)).wait_recv()
     for c in copies:
         c.wait_send()
-    for c in local:
-        c.wait()
 
 
 def align_kernel(alen, tlen, pick, stat, lp_ref, out_ref):
@@ -186,13 +198,19 @@
         last = alen[q] - 1
         first = jnp.where(lane == 0, lp_ref[q, 0:1, :], NEG)
 
-        def advance(t, carry):
-            cur, best = carry
-            moved = jnp.where(lane == 0, NEG, pltpu.roll(cur, 1, 1))
-            cur = jnp.maximum(cur, moved) + lp_ref[q, pl.ds(t, 1), :]
-            return cur, jnp.where(last == t, cur, best)
-
-        best = lax.fori_loop(1, frames, advance, (first, first), unroll=4)[1]
+        def block(t, steps, cur, best):
+            emit = [lp_ref[q, pl.ds(t + i, 1), :] for i in range(steps)]
+            rolled = [[e if c == 0 else pltpu.roll(e, c, 1) for c in range(steps - i)] for i, e in enumerate(emit)]
+            moved = [cur] + [jnp.where(lane < c, NEG, pltpu.roll(cur, c, 1)) for c in range(1, steps + 1)]
+            for i in range(steps):
+                moved = [jnp.maximum(moved[c], moved[c + 1]) + rolled[i][c] for c in range(steps - i)]
+                best = jnp.where(last == t + i, moved[0], best)
+            return moved[0], best
+
+        whole = (frames - 1) // run
+        cur, best = lax.fori_loop(0, whole, lambda i, c: block(1 + i * run, run, *c), (first, first))
+        if (frames - 1) % run:
+            best = block(1 + whole * run, (frames - 1) % run, cur, best)[1]
         score = jnp.sum(jnp.where(lane == tlen[q] - 1, best, 0.0), 1, keepdims=True)
         out_ref[q] = jnp.broadcast_to(score, (8, 128))
 
@@ -260,18 +278,22 @@
         name="score",
     )(base, xg.reshape(total, frames, width), wg, lg.reshape(total, 1, slots))
 
-    n = b * V
-    pick = pick.reshape(n, own, frames, slots)
-    stat = stat.reshape(n, own, 8, frames)
+    n = b * (V // 2)
+    pick = pick.reshape(n, 2, own, frames, slots)
+    stat = stat.reshape(n, 2, own, 8, frames)
+    picked = (n, own, frames, slots)
+    stats = (n, own, 8, frames)
     po, so = pl.pallas_call(
         functools.partial(exchange_kernel, a, b, V),
         out_shape=(
-            jax.ShapeDtypeStruct(pick.shape, pick.dtype),
-            jax.ShapeDtypeStruct(stat.shape, stat.dtype),
+            jax.ShapeDtypeStruct(picked, pick.dtype),
+            jax.ShapeDtypeStruct(stats, stat.dtype),
         ),
         in_specs=[vmem] * 2,
         out_specs=(vmem, vmem),
-        scratch_shapes=[dma((n - 1,))] * 4 + [dma((2,))],
+        scratch_shapes=[pltpu.VMEM(picked, pick.dtype), pltpu.VMEM(stats, stat.dtype)] * 2
+        + [dma((n,))] * 4
+        + [dma((n - 1,))] * 4,
         compiler_params=pltpu.CompilerParams(collective_id=1, has_side_effects=True),
         name="exchange",
     )(pick, stat)

time: 147 us -> 129 us (0.88)
  Pallas kernels: 144 us -> 125 us
    pallas_call x1, Pallas kernels: 15.4 us -> 4.8 us  [body(): pl.pallas_call(align_kernel, out_shape=(jax.ShapeDtypeStruct((own, frames...]
    pallas_call x1, Pallas kernels: 36.7 us -> 28.7 us  [body(): pl.pallas_call(functools.partial(exchange_kernel, a, b, V), out_shape=(ja...]
where the time goes in v2:
time: 129 us; the launch traced here: 128 us
  Pallas kernels  125 us (97%)
  between operations  1.96 us (2%)
    pallas_call x1, Pallas kernels, body(): pl.pallas_call(functools.partial(gather_kernel, a, b, V), out_shape=(jax....  62.6 us
    pallas_call x1, Pallas kernels, body(): pl.pallas_call(functools.partial(score_kernel, recs, tile), grid=(total /...  29.2 us
    pallas_call x1, Pallas kernels, body(): pl.pallas_call(functools.partial(exchange_kernel, a, b, V), out_shape=(ja...  28.7 us
    pallas_call x1, Pallas kernels, body(): pl.pallas_call(align_kernel, out_shape=(jax.ShapeDtypeStruct((own, frames...  4.8 us

profile of v2, /device:TPU:11, one launch (start us, length us, event | category | flops | bytes accessed | tf_op | source)
XLA Modules:
  0.0 128.4 jit_solution(12115947750742424933)
XLA Ops:
  0.6 62.6 %gather.1 = (bf16[4,4,192,1280]{3,2,1,0:T(8,128)(2,1)}, bf16[2,1280,1024]{2,1,0:T(8,128)(2,1)}, s32[4,4,1,128]{3,2,1,0:T(1,128)}) custom-call(bf16[4,192,1280]{2,1,0:T(8,128)(2,1)} %x.1, bf16[1280,1024]{1,0:T(8,128)(2,1)} %w.1, s32[4,1,128]{2,1,0:T(1,128)} %bitcast.11), custom_call_target="tpu_custom_call" | custom-call | tf_op jit(solution)/shard_map/gather/pallas_call | solution.py:237
  63.3 29.2 %score.1 = (bf16[16,192,128]{2,1,0:T(8,128)(2,1)}, f32[16,8,192]{2,1,0:T(8,128)}) custom-call(s32[1]{0:T(128)} %bitcast.base_ref, bf16[16,192,1280]{2,1,0:T(8,128)(2,1)} %bitcast.7, bf16[2,1280,1024]{2,1,0:T(8,128)(2,1)} %get-tuple-element.12.w_ref, s32[16,1,128]{2,1,0:T(1,128)} %bitcast.10), custom_call_target="tpu_custom_call" | custom-call | tf_op jit(solution)/shard_map/score/pallas_call | solution.py:259
  92.5 28.7 %exchange.1 = (bf16[8,1,192,128]{3,2,1,0:T(8,128)(2,1)}, f32[8,1,8,192]{3,2,1,0:T(8,128)}) custom-call(bf16[8,2,1,192,128]{4,3,2,1,0:T(8,128)(2,1)} %bitcast.8, f32[8,2,1,8,192]{4,3,2,1,0:T(8,128)} %bitcast.9), custom_call_target="tpu_custom_call" | custom-call | tf_op jit(solution)/shard_map/exchange/pallas_call | solution.py:286
  122.5 4.8 %align.1 = (f32[1,192,128]{2,1,0:T(8,128)}, f32[1,8,128]{2,1,0:T(8,128)}) custom-call(s32[1]{0:T(128)S(6)} %copy.7.alen, s32[1]{0:T(128)S(6)} %copy.8.tlen, bf16[8,1,192,128]{3,2,1,0:T(8,128)(2,1)} %get-tuple-element.16.pick, f32[8,1,8,192]{3,2,1,0:T(8,128)} %get-tuple-element.17.stat), custom_call_target="tpu_custom_call" | custom-call | tf_op jit(solution)/shard_map/align/pallas_call | solution.py:301
  127.3 1.2 slice.3
